TPU v7x, 32 devices: a whole 2x2x4 slice. The times are simulated.
32 devices in a mesh: blk: 8 (over z, x), ga: 4 (over y, core).
Axes of the slice: x: 2, y: 2, z: 4, core: 2. Of those that a mesh axis runs over, the one named last changes fastest.
Arguments:
- pair_val: bfloat16 [16, 16, 16, 2048], P('blk', None, None, 'ga'), may hold values from -0.125 to 0.125
- pair_con: bfloat16 [16, 16, 16, 2048], P('blk', None, None, 'ga'), may hold values from -6 to 6
- screened: bfloat16 [16, 2048, 2048], P('blk', None, 'ga'), may hold values from -0.125 to 0.125
- amplitude: bfloat16 [16, 16], P('blk'), may hold values from -6 to 6
- qmap: int32 [16, 16], P('blk'), may hold values from 0 to 15, as said below
Outputs:
- kernel_x: float32 [16, 16], P('blk')
Inputs may be any that keep to these rules, and one draw needn't show every extreme that they name: qmap[k, k'] is the label of the difference k - k' (periodic) on a grid of 8 by 2 points, with the points and the differences labelled at random; every row and every column holds each label once.
All inputs are finite; a program needn't handle non-finite values.
Results may differ from a plain program's by a relative error of at most 0.004.
Values may be sent and summed in bfloat16 or wider, within the bound.
No kernel may reach another device: no remote copies, remote signals or barrier semaphores. Data moves between devices by JAX's collectives and lax.ppermute only.
A program may use at most 64 MiB of HBM per device.

v0:
```python
import jax
import jax.numpy as jnp
from jax import lax
from jax.sharding import PartitionSpec as P

NV = 4
NC = 4


def inverse_rows(qmap):
    total = qmap.shape[1]
    labels = jnp.arange(total, dtype=jnp.int32)
    hits = (qmap[:, :, None] == labels[None, None, :]).astype(jnp.int32)
    return jnp.sum(hits * labels[None, :, None], axis=1)


def swap(value, axis, size, step):
    return lax.ppermute(value, axis, [(i, i ^ step) for i in range(size)])


def body_of(blk, ga):

    def body(pair_val, pair_con, screened, amplitude, qmap):
        local_k, total, band_pairs, width = pair_val.shape
        local_q = screened.shape[0]
        slot = lax.axis_index("ga")
        every_amp = lax.all_gather(amplitude, "blk", axis=0, tiled=True)
        partner = inverse_rows(qmap)
        con_sorted = jnp.take_along_axis(pair_con, partner[:, :, None, None], axis=1)
        con_sorted, every_amp = lax.optimization_barrier((con_sorted, every_amp))
        con_in = lax.all_to_all(con_sorted, "blk", split_axis=1, concat_axis=0, tiled=True)
        val_sorted = jnp.take_along_axis(pair_val, partner[:, :, None, None], axis=1)
        amp_sorted = every_amp[partner].reshape(local_k, total, NV, NC)
        val_five = val_sorted.reshape(local_k, total, NV, NV, width)
        zeta = jnp.einsum(
            "kqavg,kqvc->kqacg", val_five, amp_sorted, preferred_element_type=jnp.float32
        )
        zeta = zeta.astype(jnp.bfloat16).reshape(local_k, total, NV * NC, width)
        far = swap(con_in, "ga", ga, ga // 2)
        near = swap(con_in, "ga", ga, 1)
        zeta_in = lax.all_to_all(zeta, "blk", split_axis=1, concat_axis=0, tiled=True)
        pieces = {0: con_in, 1: near, ga // 2: far, ga // 2 + 1: swap(far, "ga", ga, 1)}
        weights = screened.reshape(local_q, ga, width, screened.shape[2])
        unit = 0.0
        for key, held in pieces.items():
            block = lax.dynamic_index_in_dim(weights, slot ^ key, 1, keepdims=False)
            unit = unit + jnp.einsum(
                "kqxg,qgh->kqxh", held, block, preferred_element_type=jnp.float32
            )
        unit = unit.astype(jnp.bfloat16).reshape(total, local_q, NC, NC, -1)
        zeta = zeta_in.reshape(total, local_q, NV, NC, -1)
        terms = jnp.einsum("kqcyg,kqayg->kac", unit, zeta, preferred_element_type=jnp.float32)
        terms = terms.reshape(blk, 1, local_k, NV * NC)
        terms = jnp.broadcast_to(terms, (blk, ga, local_k, NV * NC)).reshape(
            blk * ga, local_k, NV * NC
        )
        back = lax.all_to_all(terms, ("blk", "ga"), split_axis=0, concat_axis=0, tiled=True)
        return jnp.sum(back, 0) / total

    return body


def solution(mesh):
    placed = (
        P("blk", None, None, "ga"),
        P("blk", None, None, "ga"),
        P("blk", None, "ga"),
        P("blk", None),
        P("blk", None),
    )
    return jax.shard_map(
        body_of(mesh.shape["blk"], mesh.shape["ga"]),
        mesh=mesh,
        in_specs=placed,
        out_specs=P("blk", None),
        check_vma=False,
    )
```

profile of v0, /device:TPU:0, one launch (start us, length us, event | category | flops | bytes accessed | tf_op | source)
XLA Modules:
  0.0 74.7 jit_solution(2706167675406388047)
XLA Ops:
  0.0 0.0 copy-start
  0.0 0.8 %select_reduce_fusion = s32[2,16]{1,0:T(2,128)S(1)} fusion(s32[2,16]{1,0:T(2,128)} %param.11), kind=kLoop, calls=%fused_computation.24 | loop fusion | flops 1504 | bytes 256 | tf_op jit(solution)/shard_map/reduce_sum | solution.py:14
  0.9 0.1 reshape.99
  0.9 0.1 copy-done
  1.1 0.6 gather_fusion.2
  1.7 1.7 %gather_fusion.1 = bf16[32,16,512]{2,1,0:T(8,128)(2,1)S(1)} fusion(bf16[2,16,16,512]{3,2,1,0:T(8,128)(2,1)} %param.8, s32[32]{0:T(128)S(1)} %reshape.99), kind=kCustom, calls=%fused_computation.clone | custom fusion | bytes 1048832 | tf_op jit(solution)/shard_map/jit(take_along_axis)/gather | solution.py:29
  3.4 22.4 %all-gather = bf16[8,2,16]{2,1,0:T(2,128)(2,1)S(1)} all-gather(bf16[1,2,16]{2,1,0:T(2,128)(2,1)} %bitcast.98), channel_id=1, replica_groups=mesh['blk'=8,'ga'=4] {'blk'}, dimensions={0}, use_global_device_ids=true | all-gather | bytes 576 | tf_op jit(solution)/shard_map/all_gather | solution.py:27
  25.8 0.2 broadcast_select_fusion
  26.0 0.8 %copy.96 = bf16[2,16,16,512]{3,2,0,1:T(8,128)(2,1)} copy(bf16[2,16,16,512]{3,2,1,0:T(8,128)(2,1)S(1)} %get-tuple-element.9) | data formatting | bytes 1048576 | tf_op jit(solution)/shard_map/optimization_barrier | solution.py:30
  26.8 3.5 %all-to-all-start.1 = ((bf16[2,16,16,512]{3,2,0,1:T(8,128)(2,1)}), bf16[2,16,16,512]{3,2,0,1:T(8,128)(2,1)S(1)}, u32[]{:S(2)}, u32[]{:S(2)}) async-start(bf16[2,16,16,512]{3,2,0,1:T(8,128)(2,1)} %copy.96), calls=%async_computation.1 | async-start | bytes 1048576 | tf_op jit(solution)/shard_map/all_to_all | solution.py:31
  30.3 0.1 reshape.78
  30.4 0.6 gather_fusion
  31.0 0.1 copy.90
  31.1 0.1 reshape.56
  31.1 0.1 copy.107
  31.3 0.1 reshape.57
  31.4 0.4 fusion.2
  31.8 0.1 reshape.58
  32.0 0.8 %copy.92 = bf16[2,16,16,512]{3,2,0,1:T(8,128)(2,1)} copy(bf16[2,16,16,512]{3,2,1,0:T(8,128)(2,1)S(1)} %reshape.58) | data formatting | bytes 1048576 | tf_op jit(solution)/shard_map/reshape | solution.py:38
  32.8 8.4 %all-to-all-done.1 = bf16[2,16,16,512]{3,2,0,1:T(8,128)(2,1)S(1)} async-done(((bf16[2,16,16,512]{3,2,0,1:T(8,128)(2,1)}), bf16[2,16,16,512]{3,2,0,1:T(8,128)(2,1)S(1)}, u32[]{:S(2)}, u32[]{:S(2)}) %all-to-all-start.1) | async-done | bytes 524320 | tf_op jit(solution)/shard_map/all_to_all | solution.py:31
  41.2 3.7 %all-to-all-start = ((bf16[2,16,16,512]{3,2,0,1:T(8,128)(2,1)}), bf16[2,16,16,512]{3,2,0,1:T(8,128)(2,1)S(1)}, u32[]{:S(2)}, u32[]{:S(2)}) async-start(bf16[2,16,16,512]{3,2,0,1:T(8,128)(2,1)} %copy.92), calls=%async_computation | async-start | bytes 1048576 | tf_op jit(solution)/shard_map/all_to_all | solution.py:41
  45.0 1.6 %collective-permute-start.1 = (bf16[16,2,16,512]{3,2,0,1:T(8,128)(2,1)S(1)}, bf16[16,2,16,512]{3,2,0,1:T(8,128)(2,1)S(1)}, u32[]{:S(2)}, u32[]{:S(2)}) collective-permute-start(bf16[16,2,16,512]{3,2,0,1:T(8,128)(2,1)S(1)} %bitcast.92), channel_id=1, source_target_pairs={{0,2},{1,3},{2,0},{3,1},{4,6},{5,7},{6,4},{7,5},{8,10},{9,11},{10,... | collective-permute-start | bytes 1572872 | tf_op jit(solution)/shard_map/ppermute | solution.py:18
  46.5 0.0 collective-permute-start
  46.5 10.8 %all-to-all-done = bf16[2,16,16,512]{3,2,0,1:T(8,128)(2,1)S(1)} async-done(((bf16[2,16,16,512]{3,2,0,1:T(8,128)(2,1)}), bf16[2,16,16,512]{3,2,0,1:T(8,128)(2,1)S(1)}, u32[]{:S(2)}, u32[]{:S(2)}) %all-to-all-start) | async-done | bytes 524320 | tf_op jit(solution)/shard_map/all_to_all | solution.py:41
  57.3 0.5 copy.94
  57.9 0.0 copy-start.1
  57.9 1.8 %fusion.6 = f32[2,512,16,16]{1,3,2,0:T(8,128)S(1)} fusion(bf16[16,2,16,512]{3,2,0,1:T(8,128)(2,1)S(1)} %bitcast.94, bf16[2,4,512,512]{3,2,1,0:T(8,128)(2,1)} %bitcast.99, s32[]{:T(128)S(6)} %select_n.30), kind=kOutput, calls=%fused_computation.14 | convolution fusion | flops 268435456 | bytes 2621444 | tf_op jit(solution)/shard_map/kqxg,qgh->kqxh/dot_general | solution.py:47
  59.7 0.0 collective-permute-done.1
  59.7 0.1 collective-permute-start.2
  59.8 0.0 collective-permute-done
  59.8 0.6 copy-done.1
  60.4 0.4 convolution_add_fusion.2
  60.9 0.5 convolution_add_fusion.1
  61.3 0.4 collective-permute-done.2
  61.7 0.4 fusion.1
  62.2 0.1 reshape.61
  62.3 0.9 %convolution_bitcast_fusion = f32[16,4,4]{2,1,0:T(4,128)S(1)} fusion(bf16[16,2,4,4,512]{4,3,2,0,1:T(4,128)(2,1)S(1)} %reshape.61, bf16[16,2,4,4,512]{4,1,3,2,0:T(2,128)(2,1)S(1)} %bitcast.95), kind=kOutput, calls=%fused_computation.10 | convolution fusion | flops 2097152 | bytes 1049600 | tf_op jit(solution)/shard_map/kqcyg,kqayg->kac/dot_general | solution.py:52
  63.2 0.1 broadcast_in_dim.22
  63.3 10.8 %all_to_all.38 = f32[32,2,16]{2,1,0:T(2,128)S(1)} all-to-all(f32[32,2,16]{2,1,0:T(2,128)S(1)} %copy.105), channel_id=1, replica_groups=mesh['blk'=8,'ga'=4] {'blk','ga'}, dimensions={0} | all-to-all | bytes 8192 | tf_op jit(solution)/shard_map/all_to_all | solution.py:57
  74.2 0.6 broadcast_multiply_fusion
  (8 shorter events, 0.1 us)
Async XLA Ops:
  0.0 1.1 %copy-start = (bf16[2,16,16,512]{3,2,1,0:T(8,128)(2,1)S(1)}, bf16[2,16,16,512]{3,2,1,0:T(8,128)(2,1)}, u32[]{:S(2)}) copy-start(bf16[2,16,16,512]{3,2,1,0:T(8,128)(2,1)} %param.7) | copy-start | bytes 1572868
  26.8 14.4 %all-to-all-start.1 = ((bf16[2,16,16,512]{3,2,0,1:T(8,128)(2,1)}), bf16[2,16,16,512]{3,2,0,1:T(8,128)(2,1)S(1)}, u32[]{:S(2)}, u32[]{:S(2)}) async-start(bf16[2,16,16,512]{3,2,0,1:T(8,128)(2,1)} %copy.96), calls=%async_computation.1 | async-start | bytes 1048576 | tf_op jit(solution)/shard_map/all_to_all | solution.py:31
  41.2 16.1 %all-to-all-start = ((bf16[2,16,16,512]{3,2,0,1:T(8,128)(2,1)}), bf16[2,16,16,512]{3,2,0,1:T(8,128)(2,1)S(1)}, u32[]{:S(2)}, u32[]{:S(2)}) async-start(bf16[2,16,16,512]{3,2,0,1:T(8,128)(2,1)} %copy.92), calls=%async_computation | async-start | bytes 1048576 | tf_op jit(solution)/shard_map/all_to_all | solution.py:41
  45.0 14.8 %collective-permute-start.1 = (bf16[16,2,16,512]{3,2,0,1:T(8,128)(2,1)S(1)}, bf16[16,2,16,512]{3,2,0,1:T(8,128)(2,1)S(1)}, u32[]{:S(2)}, u32[]{:S(2)}) collective-permute-start(bf16[16,2,16,512]{3,2,0,1:T(8,128)(2,1)S(1)} %bitcast.92), channel_id=1, source_target_pairs={{0,2},{1,3},{2,0},{3,1},{4,6},{5,7},{6,4},{7,5},{8,10},{9,11},{10,... | collective-permute-start | bytes 1572872 | tf_op jit(solution)/shard_map/ppermute | solution.py:18
  46.5 13.3 %collective-permute-start = (bf16[16,2,16,512]{3,2,0,1:T(8,128)(2,1)S(1)}, bf16[16,2,16,512]{3,2,0,1:T(8,128)(2,1)S(1)}, u32[]{:S(2)}, u32[]{:S(2)}) collective-permute-start(bf16[16,2,16,512]{3,2,0,1:T(8,128)(2,1)S(1)} %bitcast.93), channel_id=1, source_target_pairs={{0,1},{1,0},{2,3},{3,2},{4,5},{5,4},{6,7},{7,6},{8,9},{9,8},{10,11... | collective-permute-start | bytes 1572872 | tf_op jit(solution)/shard_map/ppermute | solution.py:18
  57.9 2.5 %copy-start.1 = (bf16[2,2048,512]{2,1,0:T(8,128)(2,1)S(1)}, bf16[2,2048,512]{2,1,0:T(8,128)(2,1)}, u32[]{:S(2)}) copy-start(bf16[2,2048,512]{2,1,0:T(8,128)(2,1)} %param.9) | copy-start | bytes 12582916
  59.7 2.0 %collective-permute-start.2 = (bf16[16,2,16,512]{3,2,0,1:T(8,128)(2,1)S(1)}, bf16[16,2,16,512]{3,2,0,1:T(8,128)(2,1)S(1)}, u32[]{:S(2)}, u32[]{:S(2)}) collective-permute-start(bf16[16,2,16,512]{3,2,0,1:T(8,128)(2,1)S(1)} %collective-permute-done.1), channel_id=1, source_target_pairs={{0,1},{1,0},{2,3},{3,2},{4,5},{5,4},{6,7},{7,6},{8,9},{9,8},{10,11... | collective-permute-start | bytes 1572872 | tf_op jit(solution)/shard_map/ppermute | solution.py:18
where the time goes:
time: 75.1 us; the launch traced here: 74.7 us
  blocking collectives  33.2 us (44%)
  waiting for transfers between devices  19.6 us (26%)
  starting transfers between devices  8.84 us (12%)
  local copies, waits for them, and re-layouts  6.81 us (9%)
  matrix products  4.45 us (6%)
  other arithmetic  1.62 us (2%)
    all_gather x1, blocking collectives, body(): every_amp = lax.all_gather(amplitude, 'blk', axis=0, tiled=True)  22.4 us
    all_to_all x1, waiting for transfers between devices, body(): lax.all_to_all(zeta, 'blk', split_axis=1, concat_axis=0, tiled=True)  10.8 us
    all_to_all x1, blocking collectives, body(): lax.all_to_all(terms, ('blk', 'ga'), split_axis=0, concat_axis=0, tiled=T...  10.8 us
    all_to_all x1, waiting for transfers between devices, body(): lax.all_to_all(con_sorted, 'blk', split_axis=1, concat_axis=0, tiled=True)  8.4 us
    all_to_all x1, starting transfers between devices, body(): lax.all_to_all(zeta, 'blk', split_axis=1, concat_axis=0, tiled=True)  3.69 us
    all_to_all x1, starting transfers between devices, body(): lax.all_to_all(con_sorted, 'blk', split_axis=1, concat_axis=0, tiled=True)  3.49 us
    dot_general x4, matrix products, body(): jnp.einsum('kqxg,qgh->kqxh', held, block, preferred_element_type=jnp.floa...  3.15 us
    gather x2, local copies, waits for them, and re-layouts, body(): jnp.take_along_axis(pair_con, partner[:, :, None, None], axis=1)  1.75 us
  transfers between devices with their start and end apart: 5, of which 3 were waited for; matrix products, arithmetic and copies ran while one was open for 8% of the time, Pallas kernels for 0%

commit v1 on v0

--- a/solution.py
+++ b/solution.py
@@ -21,6 +21,13 @@
 def body_of(blk, ga):
 
     def body(pair_val, pair_con, screened, amplitude, qmap):
+
+        def lots_all_close(load):
+            return jnp.concatenate(
+                lax.all_to_all(jnp.stack(jnp.split(load, lax.axis_size("blk"), 1), 0), "blk", 0, 0),
+                0,
+            )
+
         local_k, total, band_pairs, width = pair_val.shape
         local_q = screened.shape[0]
         slot = lax.axis_index("ga")
@@ -38,7 +45,7 @@
         zeta = zeta.astype(jnp.bfloat16).reshape(local_k, total, NV * NC, width)
         far = swap(con_in, "ga", ga, ga // 2)
         near = swap(con_in, "ga", ga, 1)
-        zeta_in = lax.all_to_all(zeta, "blk", split_axis=1, concat_axis=0, tiled=True)
+        zeta_in = lots_all_close(zeta)
         pieces = {0: con_in, 1: near, ga // 2: far, ga // 2 + 1: swap(far, "ga", ga, 1)}
         weights = screened.reshape(local_q, ga, width, screened.shape[2])
         unit = 0.0

time: 75.1 us -> 73.9 us (0.984)
  waiting for transfers between devices: 19.6 us -> 15.8 us
  local copies, waits for them, and re-layouts: 6.81 us -> 10.5 us
  blocking collectives: 33.2 us -> 32.2 us
    ppermute x3, waiting for transfers between devices: 0.4 us -> 7.51 us  [swap(): return lax.ppermute(value, axis, [(i, i ^ step) for i in range(size)])]
    all_to_all x1, waiting for transfers between devices: 10.8 us -> 3.98 us  [lots_all_close(): lax.all_to_all(jnp.stack(jnp.split(load, lax.axis_size('blk'), 1), 0), 'b...]
    unnamed x4 -> x11, local copies, waits for them, and re-layouts: 0.7 us -> 4.91 us
    all_to_all x1, waiting for transfers between devices: 8.4 us -> 4.29 us  [body(): lax.all_to_all(con_sorted, 'blk', split_axis=1, concat_axis=0, tiled=True)]
    all_to_all x1, blocking collectives: 10.8 us -> 9.78 us  [body(): lax.all_to_all(terms, ('blk', 'ga'), split_axis=0, concat_axis=0, tiled=T...]
  transfers between devices with their start and end apart: 5 -> 5, of which waited for: 3 -> 4; matrix products, arithmetic and copies ran while one was open for 8% -> 14% of each run, Pallas kernels for 0% -> 0%
where the time goes in v1:
time: 73.9 us; the launch traced here: 73.6 us
  blocking collectives  32.2 us (44%)
  waiting for transfers between devices  15.8 us (21%)
  local copies, waits for them, and re-layouts  10.5 us (14%)
  starting transfers between devices  8.84 us (12%)
  matrix products  4.44 us (6%)
  other arithmetic  1.62 us (2%)
    all_gather x1, blocking collectives, body(): every_amp = lax.all_gather(amplitude, 'blk', axis=0, tiled=True)  22.4 us
    all_to_all x1, blocking collectives, body(): lax.all_to_all(terms, ('blk', 'ga'), split_axis=0, concat_axis=0, tiled=T...  9.78 us
    ppermute x3, waiting for transfers between devices, swap(): return lax.ppermute(value, axis, [(i, i ^ step) for i in range(size)])  7.51 us
    unnamed x11, local copies, waits for them, and re-layouts  4.91 us
    all_to_all x1, waiting for transfers between devices, body(): lax.all_to_all(con_sorted, 'blk', split_axis=1, concat_axis=0, tiled=True)  4.29 us
    all_to_all x1, waiting for transfers between devices, lots_all_close(): lax.all_to_all(jnp.stack(jnp.split(load, lax.axis_size('blk'), 1), 0), 'b...  3.98 us
    all_to_all x1, starting transfers between devices, lots_all_close(): lax.all_to_all(jnp.stack(jnp.split(load, lax.axis_size('blk'), 1), 0), 'b...  3.69 us
    all_to_all x1, starting transfers between devices, body(): lax.all_to_all(con_sorted, 'blk', split_axis=1, concat_axis=0, tiled=True)  3.49 us
  transfers between devices with their start and end apart: 5, of which 4 were waited for; matrix products, arithmetic and copies ran while one was open for 14% of the time, Pallas kernels for 0%

profile of v1, /device:TPU:0, one launch (start us, length us, event | category | flops | bytes accessed | tf_op | source)
XLA Modules:
  0.0 73.6 jit_solution(2614057251054318481)
XLA Ops:
  0.0 0.0 copy-start
  0.0 0.8 %select_reduce_fusion = s32[2,16]{1,0:T(2,128)S(1)} fusion(s32[2,16]{1,0:T(2,128)} %param.11), kind=kLoop, calls=%fused_computation.40 | loop fusion | flops 1504 | bytes 256 | tf_op jit(solution)/shard_map/reduce_sum | solution.py:14
  0.9 0.1 reshape.94
  0.9 0.1 copy-done
  1.1 0.6 gather_fusion.2
  1.7 1.7 %gather_fusion.1 = bf16[32,16,512]{2,1,0:T(8,128)(2,1)S(1)} fusion(bf16[2,16,16,512]{3,2,1,0:T(8,128)(2,1)} %param.8, s32[32]{0:T(128)S(1)} %reshape.94), kind=kCustom, calls=%fused_computation.clone | custom fusion | bytes 1048832 | tf_op jit(solution)/shard_map/jit(take_along_axis)/gather | solution.py:36
  3.4 22.4 %all-gather = bf16[8,2,16]{2,1,0:T(2,128)(2,1)S(1)} all-gather(bf16[1,2,16]{2,1,0:T(2,128)(2,1)} %bitcast.135), channel_id=1, replica_groups=mesh['blk'=8,'ga'=4] {'blk'}, dimensions={0}, use_global_device_ids=true | all-gather | bytes 576 | tf_op jit(solution)/shard_map/all_gather | solution.py:34
  25.8 0.2 broadcast_select_fusion
  26.0 0.8 %copy.119 = bf16[2,16,16,512]{3,2,0,1:T(8,128)(2,1)} copy(bf16[2,16,16,512]{3,2,1,0:T(8,128)(2,1)S(1)} %get-tuple-element.9) | data formatting | bytes 1048576 | tf_op jit(solution)/shard_map/optimization_barrier | solution.py:37
  26.8 3.5 %all-to-all-start.1 = ((bf16[2,16,16,512]{3,2,0,1:T(8,128)(2,1)}), bf16[2,16,16,512]{3,2,0,1:T(8,128)(2,1)S(1)}, u32[]{:S(2)}, u32[]{:S(2)}) async-start(bf16[2,16,16,512]{3,2,0,1:T(8,128)(2,1)} %copy.119), calls=%async_computation.1 | async-start | bytes 1048576 | tf_op jit(solution)/shard_map/all_to_all | solution.py:38
  30.3 0.1 reshape.73
  30.4 0.6 gather_fusion
  31.0 0.1 copy.108
  31.1 0.1 reshape.52
  31.1 0.1 copy.130
  31.3 0.1 reshape.53
  31.4 0.4 fusion.2
  31.8 0.3 copy.139
  32.1 0.7 fusion.21
  32.8 0.7 fusion.20
  33.5 0.7 fusion.19
  34.2 0.7 fusion.18
  34.9 0.7 fusion.17
  35.5 0.7 fusion.16
  36.2 0.7 fusion.15
  36.9 4.3 %all-to-all-done.1 = bf16[2,16,16,512]{3,2,0,1:T(8,128)(2,1)S(1)} async-done(((bf16[2,16,16,512]{3,2,0,1:T(8,128)(2,1)}), bf16[2,16,16,512]{3,2,0,1:T(8,128)(2,1)S(1)}, u32[]{:S(2)}, u32[]{:S(2)}) %all-to-all-start.1) | async-done | bytes 524320 | tf_op jit(solution)/shard_map/all_to_all | solution.py:38
  41.3 0.1 collective-permute-start
  41.3 1.6 %collective-permute-start.1 = (bf16[16,2,16,512]{3,2,0,1:T(8,128)(2,1)S(1)}, bf16[16,2,16,512]{3,2,0,1:T(8,128)(2,1)S(1)}, u32[]{:S(2)}, u32[]{:S(2)}) collective-permute-start(bf16[16,2,16,512]{3,2,0,1:T(8,128)(2,1)S(1)} %bitcast.131), channel_id=1, source_target_pairs={{0,2},{1,3},{2,0},{3,1},{4,6},{5,7},{6,4},{7,5},{8,10},{9,11},{10,... | collective-permute-start | bytes 1572872 | tf_op jit(solution)/shard_map/ppermute | solution.py:18
  42.9 0.7 fusion.14
  43.6 3.7 %all-to-all-start = ((bf16[8,2,2,16,512]{4,2,3,1,0:T(2,128)(2,1)}), bf16[8,2,2,16,512]{4,2,3,1,0:T(2,128)(2,1)S(1)}, u32[]{:S(2)}, u32[]{:S(2)}) async-start(bf16[8,2,2,16,512]{4,2,3,1,0:T(2,128)(2,1)} %fusion.14), calls=%async_computation | async-start | bytes 1048576 | tf_op jit(solution)/shard_map/all_to_all | solution.py:27
  47.3 0.0 copy-start.1
  47.3 1.8 %fusion.6 = f32[2,512,16,16]{1,3,2,0:T(8,128)S(1)} fusion(bf16[16,2,16,512]{3,2,0,1:T(8,128)(2,1)S(1)} %bitcast.132, bf16[2,4,512,512]{3,2,1,0:T(8,128)(2,1)} %bitcast.136, s32[]{:T(128)S(6)} %select_n.30), kind=kOutput, calls=%fused_computation.14 | convolution fusion | flops 268435456 | bytes 2621444 | tf_op jit(solution)/shard_map/kqxg,qgh->kqxh/dot_general | solution.py:54
  49.1 6.5 %collective-permute-done.1 = bf16[16,2,16,512]{3,2,0,1:T(8,128)(2,1)S(1)} collective-permute-done((bf16[16,2,16,512]{3,2,0,1:T(8,128)(2,1)S(1)}, bf16[16,2,16,512]{3,2,0,1:T(8,128)(2,1)S(1)}, u32[]{:S(2)}, u32[]{:S(2)}) %collective-permute-start.1) | collective-permute-done | bytes 524320 | tf_op jit(solution)/shard_map/ppermute | solution.py:18
  55.7 0.0 collective-permute-start.2
  55.7 0.0 collective-permute-done
  55.7 0.0 copy-done.1
  55.7 0.5 convolution_add_fusion.2
  56.1 0.4 convolution_add_fusion.1
  56.6 1.0 %collective-permute-done.2 = bf16[16,2,16,512]{3,2,0,1:T(8,128)(2,1)S(1)} collective-permute-done((bf16[16,2,16,512]{3,2,0,1:T(8,128)(2,1)S(1)}, bf16[16,2,16,512]{3,2,0,1:T(8,128)(2,1)S(1)}, u32[]{:S(2)}, u32[]{:S(2)}) %collective-permute-start.2) | collective-permute-done | bytes 524320 | tf_op jit(solution)/shard_map/ppermute | solution.py:18
  57.6 0.4 fusion.1
  58.0 0.1 reshape.56
  58.2 4.0 %all-to-all-done = bf16[8,2,2,16,512]{4,2,3,1,0:T(2,128)(2,1)S(1)} async-done(((bf16[8,2,2,16,512]{4,2,3,1,0:T(2,128)(2,1)}), bf16[8,2,2,16,512]{4,2,3,1,0:T(2,128)(2,1)S(1)}, u32[]{:S(2)}, u32[]{:S(2)}) %all-to-all-start) | async-done | bytes 524320 | tf_op jit(solution)/shard_map/all_to_all | solution.py:27
  62.1 0.9 %convolution_bitcast_fusion = f32[16,4,4]{2,1,0:T(4,128)S(1)} fusion(bf16[16,2,4,4,512]{4,3,2,0,1:T(4,128)(2,1)S(1)} %reshape.56, bf16[16,2,4,4,512]{4,1,3,2,0:T(2,128)(2,1)S(1)} %bitcast.129), kind=kOutput, calls=%fused_computation.10 | convolution fusion | flops 2097152 | bytes 1049600 | tf_op jit(solution)/shard_map/kqcyg,kqayg->kac/dot_general | solution.py:59
  63.0 0.1 broadcast_in_dim.22
  63.2 9.8 %all_to_all.28 = f32[32,2,16]{2,1,0:T(2,128)S(1)} all-to-all(f32[32,2,16]{2,1,0:T(2,128)S(1)} %copy.128), channel_id=1, replica_groups=mesh['blk'=8,'ga'=4] {'blk','ga'}, dimensions={0} | all-to-all | bytes 8192 | tf_op jit(solution)/shard_map/all_to_all | solution.py:64
  73.0 0.6 broadcast_multiply_fusion
  (8 shorter events, 0.1 us)
Async XLA Ops:
  0.0 1.1 %copy-start = (bf16[2,16,16,512]{3,2,1,0:T(8,128)(2,1)S(1)}, bf16[2,16,16,512]{3,2,1,0:T(8,128)(2,1)}, u32[]{:S(2)}) copy-start(bf16[2,16,16,512]{3,2,1,0:T(8,128)(2,1)} %param.7) | copy-start | bytes 1572868
  26.8 14.4 %all-to-all-start.1 = ((bf16[2,16,16,512]{3,2,0,1:T(8,128)(2,1)}), bf16[2,16,16,512]{3,2,0,1:T(8,128)(2,1)S(1)}, u32[]{:S(2)}, u32[]{:S(2)}) async-start(bf16[2,16,16,512]{3,2,0,1:T(8,128)(2,1)} %copy.119), calls=%async_computation.1 | async-start | bytes 1048576 | tf_op jit(solution)/shard_map/all_to_all | solution.py:38
  41.3 14.4 %collective-permute-start = (bf16[16,2,16,512]{3,2,0,1:T(8,128)(2,1)S(1)}, bf16[16,2,16,512]{3,2,0,1:T(8,128)(2,1)S(1)}, u32[]{:S(2)}, u32[]{:S(2)}) collective-permute-start(bf16[16,2,16,512]{3,2,0,1:T(8,128)(2,1)S(1)} %bitcast.130), channel_id=1, source_target_pairs={{0,1},{1,0},{2,3},{3,2},{4,5},{5,4},{6,7},{7,6},{8,9},{9,8},{10,11... | collective-permute-start | bytes 1572872 | tf_op jit(solution)/shard_map/ppermute | solution.py:18
  41.3 14.3 %collective-permute-start.1 = (bf16[16,2,16,512]{3,2,0,1:T(8,128)(2,1)S(1)}, bf16[16,2,16,512]{3,2,0,1:T(8,128)(2,1)S(1)}, u32[]{:S(2)}, u32[]{:S(2)}) collective-permute-start(bf16[16,2,16,512]{3,2,0,1:T(8,128)(2,1)S(1)} %bitcast.131), channel_id=1, source_target_pairs={{0,2},{1,3},{2,0},{3,1},{4,6},{5,7},{6,4},{7,5},{8,10},{9,11},{10,... | collective-permute-start | bytes 1572872 | tf_op jit(solution)/shard_map/ppermute | solution.py:18
  43.6 18.5 %all-to-all-start = ((bf16[8,2,2,16,512]{4,2,3,1,0:T(2,128)(2,1)}), bf16[8,2,2,16,512]{4,2,3,1,0:T(2,128)(2,1)S(1)}, u32[]{:S(2)}, u32[]{:S(2)}) async-start(bf16[8,2,2,16,512]{4,2,3,1,0:T(2,128)(2,1)} %fusion.14), calls=%async_computation | async-start | bytes 1048576 | tf_op jit(solution)/shard_map/all_to_all | solution.py:27
  47.3 8.4 %copy-start.1 = (bf16[2,2048,512]{2,1,0:T(8,128)(2,1)S(1)}, bf16[2,2048,512]{2,1,0:T(8,128)(2,1)}, u32[]{:S(2)}) copy-start(bf16[2,2048,512]{2,1,0:T(8,128)(2,1)} %param.9) | copy-start | bytes 12582916
  55.7 1.9 %collective-permute-start.2 = (bf16[16,2,16,512]{3,2,0,1:T(8,128)(2,1)S(1)}, bf16[16,2,16,512]{3,2,0,1:T(8,128)(2,1)S(1)}, u32[]{:S(2)}, u32[]{:S(2)}) collective-permute-start(bf16[16,2,16,512]{3,2,0,1:T(8,128)(2,1)S(1)} %collective-permute-done.1), channel_id=1, source_target_pairs={{0,1},{1,0},{2,3},{3,2},{4,5},{5,4},{6,7},{7,6},{8,9},{9,8},{10,11... | collective-permute-start | bytes 1572872 | tf_op jit(solution)/shard_map/ppermute | solution.py:18
